TPU v7x, 32 devices: a whole 2x2x4 slice. The times are simulated.
32 devices in a mesh: fsdp: 16 (over z, y, x), tp: 2 (over core).
Axes of the slice: x: 2, y: 2, z: 4, core: 2. Of those that a mesh axis runs over, the one named last changes fastest.
Arguments:
- inputs: bfloat16 [4096, 4096], P('fsdp'), may hold values from -6 to 6
- value_grad: bfloat16 [4096, 1024], P('fsdp', 'tp'), may hold values from -24 to 24
- value_weight: bfloat16 [4096, 1024], P('tp', 'fsdp'), may hold values from -0.09375 to 0.09375
- counts: int32 [16, 4], P('fsdp'), may hold values from 1 to 232, as said below
- offsets: int32 [16, 4], P('fsdp'), may hold values from 0 to 248, as said below
Outputs:
- input_grad: bfloat16 [4096, 4096], P('fsdp', 'tp')
- weight_grad: float32 [4096, 1024], P('fsdp', 'tp')
Inputs may be any that keep to these rules, and one draw needn't show every extreme that they name: `offsets`: on each index of fsdp the 4 samples lie in order; each starts at a multiple of 8, at or after the 8-row-aligned end of the previous one, and all lie within the 256 rows; on some index the aligned blocks of its samples fill all 256 rows. `counts`: how many rows the samples of a row group fill varies widely between indices of fsdp.
All inputs are finite; a program needn't handle non-finite values.
Results may differ from a plain program's by a relative error of at most 0.0046.
Values may be sent and summed in bfloat16 or wider, within the bound.
A program may use at most 64 MiB of HBM per device.

v0:
```python
import math
import jax
import jax.numpy as jnp
from jax import lax
from jax.sharding import PartitionSpec as P


def local(inputs, value_grad, value_weight, counts, offsets):
    tok_rows = inputs.shape[0]
    row_block = min(128, tok_rows)
    positions = jnp.arange(tok_rows, dtype=jnp.int32)[:, None]
    starts = offsets[0][None, :]
    lengths = counts[0][None, :]
    inside = (positions >= starts) & (positions < starts + lengths)
    inverse_root = lax.rsqrt(lengths.astype(jnp.float32))
    row_factor = jnp.sum(jnp.where(inside, inverse_root, jnp.zeros_like(inverse_root)), axis=1)
    scaled = (value_grad.astype(jnp.float32) * row_factor[:, None]).astype(jnp.bfloat16)
    live_end = jnp.max(offsets[0] + counts[0])
    live_blocks = (live_end + row_block - 1) // row_block
    scaled_all = lax.all_gather(scaled, "tp", axis=1, tiled=True)
    empty_inputs = jnp.zeros((tok_rows, value_weight.shape[0]), jnp.float32)
    piece = lax.all_gather(value_weight, "fsdp", axis=1, tiled=True)

    def add_add_block(block_index, partial_value):
        lower = lax.dynamic_slice_in_dim(scaled_all, block_index * row_block, row_block, 0)
        before = lax.dynamic_slice_in_dim(partial_value, block_index * row_block, row_block, 0)
        product = lax.dot_general(
            lower, piece, (((1,), (1,)), ((), ())), preferred_element_type=jnp.float32
        )
        return lax.dynamic_update_slice_in_dim(
            partial_value, before + product, block_index * row_block, 0
        )

    result = lax.fori_loop(0, live_blocks, add_add_block, empty_inputs)
    input_grad = result.astype(jnp.bfloat16)
    normalizer = 1.0 / math.sqrt(counts.shape[1] * lax.axis_size("fsdp"))
    empty = jnp.zeros((inputs.shape[1], scaled.shape[1]), jnp.float32)

    def weight_add_block(block_index, partial_value):
        feature_rows = lax.dynamic_slice_in_dim(inputs, block_index * row_block, row_block, 0)
        grad_rows = lax.dynamic_slice_in_dim(scaled, block_index * row_block, row_block, 0)
        return partial_value + lax.dot_general(
            feature_rows, grad_rows, (((0,), (0,)), ((), ())), preferred_element_type=jnp.float32
        )

    result = lax.fori_loop(0, live_blocks, weight_add_block, empty)
    summed = lax.psum_scatter(result, "fsdp", scatter_dimension=0, tiled=True)
    return (input_grad, summed * normalizer)


def solution(mesh):
    in_specs = (P("fsdp", None), P("fsdp", "tp"), P("tp", "fsdp"), P("fsdp", None), P("fsdp", None))
    out_specs = (P("fsdp", "tp"), P("fsdp", "tp"))
    return jax.shard_map(local, mesh=mesh, in_specs=in_specs, out_specs=out_specs, check_vma=False)
```

profile of v0, /device:TPU:10, one launch (start us, length us, event | category | flops | bytes accessed | tf_op | source)
XLA Modules:
  0.0 278.1 jit_solution(10683928178615963049)
XLA Ops:
  7.2 0.0 all-gather.2.cloned.1.call-start
  7.2 0.7 all-gather.2.cloned.1.call-update
  7.9 0.0 reduce-scatter.2.cloned.1.call-start
  7.9 1.3 fusion.7
  9.9 0.7 rsqrt_bitcast_fusion
  10.6 0.7 add_bitcast_fusion
  11.3 0.7 select_reduce_fusion
  12.0 1.1 multiply_convert_fusion
  13.1 0.0 copy-start
  13.1 4.3 %broadcast_in_dim.30 = f32[4096,512]{1,0:T(8,128)} broadcast(f32[]{:T(128)} %constant.38.clone.1), dimensions={} | broadcast | bytes 8388612 | tf_op jit(solution)/shard_map/broadcast_in_dim | solution.py:37
  17.4 0.0 copy-done
  17.4 8.0 %while.21 = (s32[]{:T(128)}, f32[4096,512]{1,0:T(8,128)}, s32[]{:T(128)}, bf16[256,4096]{1,0:T(8,128)(2,1)S(1)}, bf16[256,512]{1,0:T(8,128)(2,1)S(1)}, /*index=5*/s32[]{:T(128)}, s32[]{:T(128)}, s32[]{:T(128)}, s32[]{:T(128)}) while((s32[]{:T(128)}, f32[4096,512]{1,0:T(8,128)}, s32[]{:T(128)}, bf16[256,4096]{1,0:T(8,128)(2,1)S(1)}, ...), condition=%wide.region_5.6_spmd, body=%wide.region_4.5_spmd.sunk | while | flops 538968064 | bytes 17958028 | solution.py:46
  17.4 8.0 %convolution_add_fusion.3 = f32[4096,512]{1,0:T(8,128)} fusion(f32[4096,512]{1,0:T(8,128)} %get-tuple-element.191, bf16[256,4096]{1,0:T(8,128)(2,1)S(1)} %get-tuple-element.202, s32[]{:T(128)S(6)} %select_n.24, bf16[256,512]{1,0:T(8,128)(2,1)S(1)} %get-tuple-element.203), kind=kOutput, calls=%fused_computation.4.clone.1 | convolution fusion | flops 538968064 | bytes 17957888 | tf_op jit(solution)/shard_map/while/body/dot_general | solution.py:42
  25.4 0.0 reduce-scatter.2.cloned.1.call-update
  25.4 2.2 all_gather.6
  27.6 59.9 %all-gather.2.cloned.1.call-done = bf16[2048,1024]{0,1:T(8,128)(2,1)} async-done(((bf16[2048,64]{0,1:T(8,128)(2,1)}), bf16[2048,1024]{0,1:T(8,128)(2,1)}) %all-gather.2.cloned.1.call-update) | async-done | bytes 4194320 | tf_op jit(solution)/shard_map/all_gather | solution.py:22
  87.5 6.4 %copy.9 = bf16[2048,1024]{1,0:T(8,128)(2,1)} copy(bf16[2048,1024]{0,1:T(8,128)(2,1)} %all-gather.2.cloned.1.call-done) | data formatting | bytes 8388608 | tf_op jit(solution)/shard_map/while | solution.py:34
  93.9 0.2 broadcast_in_dim.26
  94.1 4.0 %while.20 = (s32[]{:T(128)}, f32[256,2048]{1,0:T(8,128)S(1)}, s32[]{:T(128)}, bf16[256,1024]{1,0:T(8,128)(2,1)S(1)}, bf16[2048,1024]{1,0:T(8,128)(2,1)}, /*index=5*/s32[]{:T(128)}, s32[]{:T(128)}, s32[]{:T(128)}, s32[]{:T(128)}) while((s32[]{:T(128)}, f32[256,2048]{1,0:T(8,128)S(1)}, s32[]{:T(128)}, bf16[256,1024]{1,0:T(8,128)(2,1)S(1)}, ...), condition=%wide.region_3.4_spmd, body=%wide.region_2.3_spmd.sunk | while | flops 537133056 | bytes 6554763 | solution.py:34
  94.2 4.0 %fusion.16 = f32[256,2048]{1,0:T(8,128)S(1)} fusion(f32[256,2048]{1,0:T(8,128)S(1)} %get-tuple-element.164, s32[]{:T(128)S(6)} %select_n.23, bf16[2048,1024]{1,0:T(8,128)(2,1)} %get-tuple-element.176, bf16[256,1024]{1,0:T(8,128)(2,1)S(1)} %get-tuple-element.175), kind=kOutput, calls=%fused_computation.1.clone.1 | convolution fusion | flops 537133056 | bytes 6554624 | tf_op jit(solution)/shard_map/while/body/dot_general | solution.py:27
  98.1 1.1 convert_element_type.15
  99.3 170.2 %reduce-scatter.2.cloned.1.call-done = f32[256,512]{1,0:T(8,128)} async-done(((f32[4096,512]{1,0:T(8,128)}), f32[256,512]{1,0:T(8,128)}) %reduce-scatter.2.cloned.1.call-update) | async-done | bytes 524304 | tf_op jit(solution)/shard_map/reduce_scatter | solution.py:47
  269.4 1.9 broadcast_multiply_fusion
Async XLA Ops:
  7.2 80.3 %all-gather.2.cloned.1.call-start = ((), (), s32[]{:S(2)}) async-start(), calls=%async_computation.1 | async-start | bytes 4456448 | tf_op jit(solution)/shard_map/all_gather | solution.py:22
  7.9 261.5 %reduce-scatter.2.cloned.1.call-start = ((), (), s32[]{:S(2)}) async-start(), calls=%async_computation.2 | async-start | bytes 8912896 | tf_op jit(solution)/shard_map/reduce_scatter | solution.py:47
  13.1 4.3 %copy-start = (bf16[256,4096]{1,0:T(8,128)(2,1)S(1)}, bf16[256,4096]{1,0:T(8,128)(2,1)}, u32[]{:S(2)}) copy-start(bf16[256,4096]{1,0:T(8,128)(2,1)} %param.9) | copy-start | bytes 6291460
Sparse Core Ops, SparseCore 0:
  10.7 76.6 all-gather.1
  89.8 179.6 reduce-scatter.1
where the time goes:
time: 279 us; the launch traced here: 278 us
  waiting for transfers between devices  231 us (83%)
  between operations  14.7 us (5%)
  matrix products  12 us (4%)
  local copies, waits for them, and re-layouts  10.9 us (4%)
  other arithmetic  7.43 us (3%)
    reduce_scatter x1, waiting for transfers between devices, local(): summed = lax.psum_scatter(result, 'fsdp', scatter_dimension=0, tiled=True)  170 us
    all_gather x1, waiting for transfers between devices, local(): piece = lax.all_gather(value_weight, 'fsdp', axis=1, tiled=True)  59.9 us
    dot_general x1, matrix products, weight_add_block(): lax.dot_general(feature_rows, grad_rows, (((0,), (0,)), ((), ())), prefer...  7.98 us
    while x1, local copies, waits for them, and re-layouts, local(): result = lax.fori_loop(0, live_blocks, add_add_block, empty_inputs)  6.42 us
  transfers between devices with their start and end apart: 2, of which 2 were waited for; matrix products, arithmetic and copies ran while one was open for 10% of the time, Pallas kernels for 0%

commit v1 on v0

--- a/solution.py
+++ b/solution.py
@@ -19,7 +19,12 @@
     live_blocks = (live_end + row_block - 1) // row_block
     scaled_all = lax.all_gather(scaled, "tp", axis=1, tiled=True)
     empty_inputs = jnp.zeros((tok_rows, value_weight.shape[0]), jnp.float32)
-    piece = lax.all_gather(value_weight, "fsdp", axis=1, tiled=True)
+    ring = [value_weight]
+    for hop in range(15):
+        ring.append(lax.ppermute(ring[-1], "fsdp", [(dev, (dev + 1) % 16) for dev in range(16)]))
+    piece = jnp.roll(
+        jnp.concatenate(ring[::-1], axis=1), (lax.axis_index("fsdp") + 1) * ring[0].shape[1], axis=1
+    )
 
     def add_add_block(block_index, partial_value):
         lower = lax.dynamic_slice_in_dim(scaled_all, block_index * row_block, row_block, 0)

time: 279 us -> 449 us (1.61)
  the two profiles are of different devices: /device:TPU:10 before, /device:TPU:16 now
where the time goes in v1:
time: 449 us; the launch traced here: 447 us
  waiting for transfers between devices  325 us (72%)
  local copies, waits for them, and re-layouts  39.6 us (9%)
  starting transfers between devices  33.9 us (8%)
  matrix products  23.2 us (5%)
  between operations  14.8 us (3%)
  other arithmetic  7.43 us (2%)
    ppermute x15, waiting for transfers between devices, local(): lax.ppermute(ring[-1], 'fsdp', [(dev, (dev + 1) % 16) for dev in range(16)])  325 us
    ppermute x15, starting transfers between devices, local(): lax.ppermute(ring[-1], 'fsdp', [(dev, (dev + 1) % 16) for dev in range(16)])  33.9 us
    concatenate x1, local copies, waits for them, and re-layouts, local(): jnp.roll(jnp.concatenate(ring[::-1], axis=1), (lax.axis_index('fsdp') + 1...  20.2 us
    dot_general x2, matrix products, weight_add_block(): lax.dot_general(feature_rows, grad_rows, (((0,), (0,)), ((), ())), prefer...  15.8 us
  transfers between devices with their start and end apart: 16, of which 15 were waited for; matrix products, arithmetic and copies ran while one was open for 8% of the time, Pallas kernels for 0%

profile of v1, /device:TPU:16, one launch (start us, length us, event | category | flops | bytes accessed | tf_op | source)
XLA Modules:
  0.0 446.5 jit_solution(11944555968389722837)
XLA Ops:
  7.2 0.0 reduce-scatter.2.cloned.1.call-start
  7.2 1.3 fusion.7
  9.2 0.7 rsqrt_bitcast_fusion
  9.8 0.7 add_bitcast_fusion
  10.5 0.7 select_reduce_fusion
  11.3 1.1 multiply_convert_fusion
  12.3 0.0 copy-start
  12.3 4.3 broadcast_in_dim.30
  16.6 0.0 copy-done
  16.6 15.8 %while.21 = (s32[]{:T(128)}, f32[4096,512]{1,0:T(8,128)}, s32[]{:T(128)}, bf16[256,4096]{1,0:T(8,128)(2,1)S(1)}, bf16[256,512]{1,0:T(8,128)(2,1)S(1)}, /*index=5*/s32[]{:T(128)}, s32[]{:T(128)}, s32[]{:T(128)}, s32[]{:T(128)}) while((s32[]{:T(128)}, f32[4096,512]{1,0:T(8,128)}, s32[]{:T(128)}, bf16[256,4096]{1,0:T(8,128)(2,1)S(1)}, ...), condition=%wide.region_5.6_spmd, body=%wide.region_4.5_spmd.sunk | while | flops 538968064 | bytes 17958028 | solution.py:51
  16.6 7.9 %convolution_add_fusion.3 = f32[4096,512]{1,0:T(8,128)} fusion(f32[4096,512]{1,0:T(8,128)} %get-tuple-element.181, bf16[256,4096]{1,0:T(8,128)(2,1)S(1)} %get-tuple-element.192, s32[]{:T(128)S(6)} %select_n.38, bf16[256,512]{1,0:T(8,128)(2,1)S(1)} %get-tuple-element.193), kind=kOutput, calls=%fused_computation.4.clone.1 | convolution fusion | flops 538968064 | bytes 17957888 | tf_op jit(solution)/shard_map/while/body/dot_general | solution.py:47
  24.5 7.9 %convolution_add_fusion.3 = f32[4096,512]{1,0:T(8,128)} fusion(f32[4096,512]{1,0:T(8,128)} %get-tuple-element.181, bf16[256,4096]{1,0:T(8,128)(2,1)S(1)} %get-tuple-element.192, s32[]{:T(128)S(6)} %select_n.38, bf16[256,512]{1,0:T(8,128)(2,1)S(1)} %get-tuple-element.193), kind=kOutput, calls=%fused_computation.4.clone.1 | convolution fusion | flops 538968064 | bytes 17957888 | tf_op jit(solution)/shard_map/while/body/dot_general | solution.py:47
  32.4 0.0 copy-start.10
  32.4 0.0 reduce-scatter.2.cloned.1.call-update
  32.4 0.9 copy-done.10
  33.3 0.3 copy.10
  33.6 0.1 collective-permute-start
  33.7 30.3 %collective-permute-done = bf16[2048,64]{1,0:T(8,128)(2,1)S(1)} collective-permute-done((bf16[2048,64]{1,0:T(8,128)(2,1)S(1)}, bf16[2048,64]{1,0:T(8,128)(2,1)S(1)}, u32[]{:S(2)}, u32[]{:S(2)}) %collective-permute-start) | collective-permute-done | bytes 262176 | tf_op jit(solution)/shard_map/ppermute | solution.py:24
  64.0 2.5 collective-permute-start.1
  66.5 32.9 %collective-permute-done.1 = bf16[2048,64]{1,0:T(8,128)(2,1)S(1)} collective-permute-done((bf16[2048,64]{1,0:T(8,128)(2,1)S(1)}, bf16[2048,64]{1,0:T(8,128)(2,1)S(1)}, u32[]{:S(2)}, u32[]{:S(2)}) %collective-permute-start.1) | collective-permute-done | bytes 262176 | tf_op jit(solution)/shard_map/ppermute | solution.py:24
  99.4 2.5 collective-permute-start.2
  101.9 32.7 %collective-permute-done.2 = bf16[2048,64]{1,0:T(8,128)(2,1)S(1)} collective-permute-done((bf16[2048,64]{1,0:T(8,128)(2,1)S(1)}, bf16[2048,64]{1,0:T(8,128)(2,1)S(1)}, u32[]{:S(2)}, u32[]{:S(2)}) %collective-permute-start.2) | collective-permute-done | bytes 262176 | tf_op jit(solution)/shard_map/ppermute | solution.py:24
  134.6 2.5 collective-permute-start.3
  137.0 34.1 %collective-permute-done.3 = bf16[2048,64]{1,0:T(8,128)(2,1)S(1)} collective-permute-done((bf16[2048,64]{1,0:T(8,128)(2,1)S(1)}, bf16[2048,64]{1,0:T(8,128)(2,1)S(1)}, u32[]{:S(2)}, u32[]{:S(2)}) %collective-permute-start.3) | collective-permute-done | bytes 262176 | tf_op jit(solution)/shard_map/ppermute | solution.py:24
  171.1 4.4 collective-permute-start.4
  175.5 31.1 %collective-permute-done.4 = bf16[2048,64]{1,0:T(8,128)(2,1)S(1)} collective-permute-done((bf16[2048,64]{1,0:T(8,128)(2,1)S(1)}, bf16[2048,64]{1,0:T(8,128)(2,1)S(1)}, u32[]{:S(2)}, u32[]{:S(2)}) %collective-permute-start.4) | collective-permute-done | bytes 262176 | tf_op jit(solution)/shard_map/ppermute | solution.py:24
  206.6 0.8 copy-done.1
  207.4 4.2 collective-permute-start.5
  211.6 31.4 %collective-permute-done.5 = bf16[2048,64]{1,0:T(8,128)(2,1)S(1)} collective-permute-done((bf16[2048,64]{1,0:T(8,128)(2,1)S(1)}, bf16[2048,64]{1,0:T(8,128)(2,1)S(1)}, u32[]{:S(2)}, u32[]{:S(2)}) %collective-permute-start.5) | collective-permute-done | bytes 262176 | tf_op jit(solution)/shard_map/ppermute | solution.py:24
  243.0 0.8 copy-done.2
  243.8 2.5 collective-permute-start.6
  246.2 33.6 %collective-permute-done.6 = bf16[2048,64]{1,0:T(8,128)(2,1)S(1)} collective-permute-done((bf16[2048,64]{1,0:T(8,128)(2,1)S(1)}, bf16[2048,64]{1,0:T(8,128)(2,1)S(1)}, u32[]{:S(2)}, u32[]{:S(2)}) %collective-permute-start.6) | collective-permute-done | bytes 262176 | tf_op jit(solution)/shard_map/ppermute | solution.py:24
  279.8 0.8 copy-done.3
  280.6 2.5 collective-permute-start.7
  283.1 13.6 %collective-permute-done.7 = bf16[2048,64]{1,0:T(8,128)(2,1)S(1)} collective-permute-done((bf16[2048,64]{1,0:T(8,128)(2,1)S(1)}, bf16[2048,64]{1,0:T(8,128)(2,1)S(1)}, u32[]{:S(2)}, u32[]{:S(2)}) %collective-permute-start.7) | collective-permute-done | bytes 262176 | tf_op jit(solution)/shard_map/ppermute | solution.py:24
  296.7 0.8 copy-done.4
  297.5 2.9 collective-permute-start.8
  300.4 10.8 %collective-permute-done.8 = bf16[2048,64]{1,0:T(8,128)(2,1)S(1)} collective-permute-done((bf16[2048,64]{1,0:T(8,128)(2,1)S(1)}, bf16[2048,64]{1,0:T(8,128)(2,1)S(1)}, u32[]{:S(2)}, u32[]{:S(2)}) %collective-permute-start.8) | collective-permute-done | bytes 262176 | tf_op jit(solution)/shard_map/ppermute | solution.py:24
  311.2 0.8 copy-done.5
  312.0 3.5 collective-permute-start.9
  315.5 11.7 %collective-permute-done.9 = bf16[2048,64]{1,0:T(8,128)(2,1)S(1)} collective-permute-done((bf16[2048,64]{1,0:T(8,128)(2,1)S(1)}, bf16[2048,64]{1,0:T(8,128)(2,1)S(1)}, u32[]{:S(2)}, u32[]{:S(2)}) %collective-permute-start.9) | collective-permute-done | bytes 262176 | tf_op jit(solution)/shard_map/ppermute | solution.py:24
  327.2 0.8 copy-done.6
  328.0 3.7 collective-permute-start.10
  331.7 12.6 %collective-permute-done.10 = bf16[2048,64]{1,0:T(8,128)(2,1)S(1)} collective-permute-done((bf16[2048,64]{1,0:T(8,128)(2,1)S(1)}, bf16[2048,64]{1,0:T(8,128)(2,1)S(1)}, u32[]{:S(2)}, u32[]{:S(2)}) %collective-permute-start.10) | collective-permute-done | bytes 262176 | tf_op jit(solution)/shard_map/ppermute | solution.py:24
  344.2 0.8 copy-done.7
  345.0 2.3 collective-permute-start.11
  347.3 13.5 %collective-permute-done.11 = bf16[2048,64]{1,0:T(8,128)(2,1)S(1)} collective-permute-done((bf16[2048,64]{1,0:T(8,128)(2,1)S(1)}, bf16[2048,64]{1,0:T(8,128)(2,1)S(1)}, u32[]{:S(2)}, u32[]{:S(2)}) %collective-permute-start.11) | collective-permute-done | bytes 262176 | tf_op jit(solution)/shard_map/ppermute | solution.py:24
  360.8 0.8 copy-done.8
  361.6 0.5 collective-permute-start.12
  362.1 14.5 %collective-permute-done.12 = bf16[2048,64]{1,0:T(8,128)(2,1)S(1)} collective-permute-done((bf16[2048,64]{1,0:T(8,128)(2,1)S(1)}, bf16[2048,64]{1,0:T(8,128)(2,1)S(1)}, u32[]{:S(2)}, u32[]{:S(2)}) %collective-permute-start.12) | collective-permute-done | bytes 262176 | tf_op jit(solution)/shard_map/ppermute | solution.py:24
  376.6 0.8 copy-done.9
  377.4 0.0 collective-permute-start.13
  377.4 13.6 %collective-permute-done.13 = bf16[2048,64]{1,0:T(8,128)(2,1)} collective-permute-done((bf16[2048,64]{1,0:T(8,128)(2,1)S(1)}, bf16[2048,64]{1,0:T(8,128)(2,1)}, u32[]{:S(2)}, u32[]{:S(2)}) %collective-permute-start.13) | collective-permute-done | bytes 262176 | tf_op jit(solution)/shard_map/ppermute | solution.py:24
  391.0 0.0 collective-permute-start.14
  391.0 2.2 all_gather.3
  393.1 9.1 %collective-permute-done.14 = bf16[2048,64]{1,0:T(8,128)(2,1)} collective-permute-done((bf16[2048,64]{1,0:T(8,128)(2,1)}, bf16[2048,64]{1,0:T(8,128)(2,1)}, u32[]{:S(2)}, u32[]{:S(2)}) %collective-permute-start.14) | collective-permute-done | bytes 262176 | tf_op jit(solution)/shard_map/ppermute | solution.py:24
  402.3 20.2 %concatenate.6 = bf16[2048,2048]{1,0:T(8,128)(2,1)} concatenate(bf16[2048,64]{1,0:T(8,128)(2,1)} %collective-permute-done.14, bf16[2048,64]{1,0:T(8,128)(2,1)} %collective-permute-done.13, bf16[2048,64]{1,0:T(8,128)(2,1)} %copy-done.9, bf16[2048,64]{1,0:T(8,128)(2,1)} %copy-done.8, bf16[2048,64]{1,0:T(8,128)(2,1)} %copy-done.7, bf16[2048,64]{1,0:T(8,128)(2,1)} %copy-done.6, ...), dimensions={1} | concatenate | bytes 16777216 | tf_op jit(solution)/shard_map/jit(_roll_dynamic)/concatenate | solution.py:25
  422.5 6.5 %constant_dynamic-slice_fusion = bf16[2048,1024]{1,0:T(8,128)(2,1)} fusion(bf16[2048,2048]{1,0:T(8,128)(2,1)} %concatenate.6, s32[]{:T(128)S(6)} %select_n.33), kind=kLoop, calls=%fused_computation.18 | loop fusion | bytes 8388612 | tf_op jit(solution)/shard_map/jit(_roll_dynamic)/dynamic_slice | solution.py:25
  428.9 0.2 broadcast_in_dim.26
  429.2 7.5 %while.20 = (s32[]{:T(128)}, f32[256,2048]{1,0:T(8,128)S(1)}, s32[]{:T(128)}, bf16[256,1024]{1,0:T(8,128)(2,1)S(1)}, bf16[2048,1024]{1,0:T(8,128)(2,1)}, /*index=5*/s32[]{:T(128)}, s32[]{:T(128)}, s32[]{:T(128)}, s32[]{:T(128)}) while((s32[]{:T(128)}, f32[256,2048]{1,0:T(8,128)S(1)}, s32[]{:T(128)}, bf16[256,1024]{1,0:T(8,128)(2,1)S(1)}, ...), condition=%wide.region_3.4_spmd, body=%wide.region_2.3_spmd.sunk | while | flops 537133056 | bytes 6554763 | solution.py:39
  429.2 3.7 fusion.16
  432.9 3.7 fusion.16
  436.7 1.1 convert_element_type.15
  437.8 1.9 broadcast_multiply_fusion
  (10 shorter events, 0.0 us)
Async XLA Ops:
  7.2 430.6 %reduce-scatter.2.cloned.1.call-start = ((), (), s32[]{:S(2)}) async-start(), calls=%async_computation.1 | async-start | bytes 8912896 | tf_op jit(solution)/shard_map/reduce_scatter | solution.py:52
  12.3 4.3 copy-start
  32.4 0.9 copy-start.10
  33.6 30.4 %collective-permute-start = (bf16[2048,64]{1,0:T(8,128)(2,1)S(1)}, bf16[2048,64]{1,0:T(8,128)(2,1)S(1)}, u32[]{:S(2)}, u32[]{:S(2)}) collective-permute-start(bf16[2048,64]{1,0:T(8,128)(2,1)S(1)} %copy.10), channel_id=1, source_target_pairs={{0,2},{2,4},{4,6},{6,8},{8,10},{10,12},{12,14},{14,16},{16,18},{18... | collective-permute-start | bytes 786440 | tf_op jit(solution)/shard_map/ppermute | solution.py:24
  64.0 35.4 %collective-permute-start.1 = (bf16[2048,64]{1,0:T(8,128)(2,1)S(1)}, bf16[2048,64]{1,0:T(8,128)(2,1)S(1)}, u32[]{:S(2)}, u32[]{:S(2)}) collective-permute-start(bf16[2048,64]{1,0:T(8,128)(2,1)S(1)} %collective-permute-done), channel_id=1, source_target_pairs={{0,2},{2,4},{4,6},{6,8},{8,10},{10,12},{12,14},{14,16},{16,18},{18... | collective-permute-start | bytes 786440 | tf_op jit(solution)/shard_map/ppermute | solution.py:24
  99.4 35.2 %collective-permute-start.2 = (bf16[2048,64]{1,0:T(8,128)(2,1)S(1)}, bf16[2048,64]{1,0:T(8,128)(2,1)S(1)}, u32[]{:S(2)}, u32[]{:S(2)}) collective-permute-start(bf16[2048,64]{1,0:T(8,128)(2,1)S(1)} %collective-permute-done.1), channel_id=1, source_target_pairs={{0,2},{2,4},{4,6},{6,8},{8,10},{10,12},{12,14},{14,16},{16,18},{18... | collective-permute-start | bytes 786440 | tf_op jit(solution)/shard_map/ppermute | solution.py:24
  134.6 36.6 %collective-permute-start.3 = (bf16[2048,64]{1,0:T(8,128)(2,1)S(1)}, bf16[2048,64]{1,0:T(8,128)(2,1)S(1)}, u32[]{:S(2)}, u32[]{:S(2)}) collective-permute-start(bf16[2048,64]{1,0:T(8,128)(2,1)S(1)} %collective-permute-done.2), channel_id=1, source_target_pairs={{0,2},{2,4},{4,6},{6,8},{8,10},{10,12},{12,14},{14,16},{16,18},{18... | collective-permute-start | bytes 786440 | tf_op jit(solution)/shard_map/ppermute | solution.py:24
  171.1 35.5 %collective-permute-start.4 = (bf16[2048,64]{1,0:T(8,128)(2,1)S(1)}, bf16[2048,64]{1,0:T(8,128)(2,1)S(1)}, u32[]{:S(2)}, u32[]{:S(2)}) collective-permute-start(bf16[2048,64]{1,0:T(8,128)(2,1)S(1)} %collective-permute-done.3), channel_id=1, source_target_pairs={{0,2},{2,4},{4,6},{6,8},{8,10},{10,12},{12,14},{14,16},{16,18},{18... | collective-permute-start | bytes 786440 | tf_op jit(solution)/shard_map/ppermute | solution.py:24
  206.6 0.8 copy-start.1
  207.4 35.6 %collective-permute-start.5 = (bf16[2048,64]{1,0:T(8,128)(2,1)S(1)}, bf16[2048,64]{1,0:T(8,128)(2,1)S(1)}, u32[]{:S(2)}, u32[]{:S(2)}) collective-permute-start(bf16[2048,64]{1,0:T(8,128)(2,1)S(1)} %collective-permute-done.4), channel_id=1, source_target_pairs={{0,2},{2,4},{4,6},{6,8},{8,10},{10,12},{12,14},{14,16},{16,18},{18... | collective-permute-start | bytes 786440 | tf_op jit(solution)/shard_map/ppermute | solution.py:24
  243.0 0.8 copy-start.2
  243.8 36.1 %collective-permute-start.6 = (bf16[2048,64]{1,0:T(8,128)(2,1)S(1)}, bf16[2048,64]{1,0:T(8,128)(2,1)S(1)}, u32[]{:S(2)}, u32[]{:S(2)}) collective-permute-start(bf16[2048,64]{1,0:T(8,128)(2,1)S(1)} %collective-permute-done.5), channel_id=1, source_target_pairs={{0,2},{2,4},{4,6},{6,8},{8,10},{10,12},{12,14},{14,16},{16,18},{18... | collective-permute-start | bytes 786440 | tf_op jit(solution)/shard_map/ppermute | solution.py:24
  279.8 0.8 copy-start.3
  280.6 16.0 %collective-permute-start.7 = (bf16[2048,64]{1,0:T(8,128)(2,1)S(1)}, bf16[2048,64]{1,0:T(8,128)(2,1)S(1)}, u32[]{:S(2)}, u32[]{:S(2)}) collective-permute-start(bf16[2048,64]{1,0:T(8,128)(2,1)S(1)} %collective-permute-done.6), channel_id=1, source_target_pairs={{0,2},{2,4},{4,6},{6,8},{8,10},{10,12},{12,14},{14,16},{16,18},{18... | collective-permute-start | bytes 786440 | tf_op jit(solution)/shard_map/ppermute | solution.py:24
  296.7 0.8 copy-start.4
  297.5 13.7 %collective-permute-start.8 = (bf16[2048,64]{1,0:T(8,128)(2,1)S(1)}, bf16[2048,64]{1,0:T(8,128)(2,1)S(1)}, u32[]{:S(2)}, u32[]{:S(2)}) collective-permute-start(bf16[2048,64]{1,0:T(8,128)(2,1)S(1)} %collective-permute-done.7), channel_id=1, source_target_pairs={{0,2},{2,4},{4,6},{6,8},{8,10},{10,12},{12,14},{14,16},{16,18},{18... | collective-permute-start | bytes 786440 | tf_op jit(solution)/shard_map/ppermute | solution.py:24
  311.2 0.8 copy-start.5
  312.0 15.2 %collective-permute-start.9 = (bf16[2048,64]{1,0:T(8,128)(2,1)S(1)}, bf16[2048,64]{1,0:T(8,128)(2,1)S(1)}, u32[]{:S(2)}, u32[]{:S(2)}) collective-permute-start(bf16[2048,64]{1,0:T(8,128)(2,1)S(1)} %collective-permute-done.8), channel_id=1, source_target_pairs={{0,2},{2,4},{4,6},{6,8},{8,10},{10,12},{12,14},{14,16},{16,18},{18... | collective-permute-start | bytes 786440 | tf_op jit(solution)/shard_map/ppermute | solution.py:24
  327.2 0.8 copy-start.6
  328.0 16.2 %collective-permute-start.10 = (bf16[2048,64]{1,0:T(8,128)(2,1)S(1)}, bf16[2048,64]{1,0:T(8,128)(2,1)S(1)}, u32[]{:S(2)}, u32[]{:S(2)}) collective-permute-start(bf16[2048,64]{1,0:T(8,128)(2,1)S(1)} %collective-permute-done.9), channel_id=1, source_target_pairs={{0,2},{2,4},{4,6},{6,8},{8,10},{10,12},{12,14},{14,16},{16,18},{18... | collective-permute-start | bytes 786440 | tf_op jit(solution)/shard_map/ppermute | solution.py:24
  344.2 0.8 copy-start.7
  345.0 15.8 %collective-permute-start.11 = (bf16[2048,64]{1,0:T(8,128)(2,1)S(1)}, bf16[2048,64]{1,0:T(8,128)(2,1)S(1)}, u32[]{:S(2)}, u32[]{:S(2)}) collective-permute-start(bf16[2048,64]{1,0:T(8,128)(2,1)S(1)} %collective-permute-done.10), channel_id=1, source_target_pairs={{0,2},{2,4},{4,6},{6,8},{8,10},{10,12},{12,14},{14,16},{16,18},{18... | collective-permute-start | bytes 786440 | tf_op jit(solution)/shard_map/ppermute | solution.py:24
  360.8 0.8 copy-start.8
  361.6 14.9 %collective-permute-start.12 = (bf16[2048,64]{1,0:T(8,128)(2,1)S(1)}, bf16[2048,64]{1,0:T(8,128)(2,1)S(1)}, u32[]{:S(2)}, u32[]{:S(2)}) collective-permute-start(bf16[2048,64]{1,0:T(8,128)(2,1)S(1)} %collective-permute-done.11), channel_id=1, source_target_pairs={{0,2},{2,4},{4,6},{6,8},{8,10},{10,12},{12,14},{14,16},{16,18},{18... | collective-permute-start | bytes 786440 | tf_op jit(solution)/shard_map/ppermute | solution.py:24
  376.6 0.8 copy-start.9
  377.4 13.6 %collective-permute-start.13 = (bf16[2048,64]{1,0:T(8,128)(2,1)S(1)}, bf16[2048,64]{1,0:T(8,128)(2,1)}, u32[]{:S(2)}, u32[]{:S(2)}) collective-permute-start(bf16[2048,64]{1,0:T(8,128)(2,1)S(1)} %collective-permute-done.12), channel_id=1, source_target_pairs={{0,2},{2,4},{4,6},{6,8},{8,10},{10,12},{12,14},{14,16},{16,18},{18... | collective-permute-start | bytes 786440 | tf_op jit(solution)/shard_map/ppermute | solution.py:24
  391.0 11.3 %collective-permute-start.14 = (bf16[2048,64]{1,0:T(8,128)(2,1)}, bf16[2048,64]{1,0:T(8,128)(2,1)}, u32[]{:S(2)}, u32[]{:S(2)}) collective-permute-start(bf16[2048,64]{1,0:T(8,128)(2,1)} %collective-permute-done.13), channel_id=1, source_target_pairs={{0,2},{2,4},{4,6},{6,8},{8,10},{10,12},{12,14},{14,16},{16,18},{18... | collective-permute-start | bytes 786440 | tf_op jit(solution)/shard_map/ppermute | solution.py:24
Sparse Core Ops, SparseCore 0:
  32.5 264.5 reduce-scatter.1
